TPU v7x, 128 devices: a whole 4x4x4 slice. The times are simulated.
128 devices in a mesh: gx: 4 (over z), gy: 4 (over y), gz: 8 (over x, core).
Axes of the slice: x: 4, y: 4, z: 4, core: 2. Of those that a mesh axis runs over, the one named last changes fastest.
Arguments:
- positions: float32 [3, 64, 64, 2048], P(None, 'gx', 'gy', 'gz'), may hold values from -6 to 6
- pair_node: int32 [4, 4, 8, 32, 256], P('gx', 'gy', 'gz'), may hold values from 0 to 255
- pair_line: int32 [4, 4, 8, 32], P('gx', 'gy', 'gz'), may hold values from 0 to 255
- pair_far: int32 [4, 4, 8, 32, 256], P('gx', 'gy', 'gz'), may hold values from 0 to 261, as said below
- far_line: int32 [4, 4, 8, 32], P('gx', 'gy', 'gz'), may hold values from 0 to 483, as said below
- pair_geom: float32 [4, 4, 8, 32, 4, 256], P('gx', 'gy', 'gz'), may hold values from -4 to 4
- live_blocks: int32 [4, 4, 8], P('gx', 'gy', 'gz'), may hold values from 8 to 32, as said below
Outputs:
- corrected: float32 [3, 64, 64, 2048], P(None, 'gx', 'gy', 'gz')
- sweep_history: float32 [2, 5], replicated
Inputs may be any that keep to these rules, and one draw needn't show every extreme that they name: `pair_far`: together with far_line: at most one of the three coordinates of node b lies outside the owner block's own nodes; node b lies inside the whole grid; in slots below 16 node b is one of the owner block's own nodes. `far_line`: together with pair_far, as stated there. `live_blocks`: some owner block has all 32 slots live.
All inputs are finite; a program needn't handle non-finite values.
Results may differ from a plain program's by a relative error of at most 0.0001.
Values sent between devices are 32-bit elements; how exact they have to be, the bound alone decides.
No kernel may reach another device: no remote copies, remote signals or barrier semaphores. Data moves between devices by JAX's collectives and lax.ppermute only.
A program may use at most 64 MiB of HBM per device.

v0:
```python
import math
import jax
import jax.numpy as jnp
from jax import lax
from jax.sharding import Mesh
from jax.sharding import PartitionSpec as P

RIM = 3
SWEEPS = 5
GZ = ("gz_0", "gz_1")
GX_GY_GZ = ("gx", "gy", "gz_0", "gz_1")
relax_factor = 0.9
highest = lax.Precision.HIGHEST


def extended(cells, sides, width):
    for axis, dim in sides:
        count = lax.axis_size(axis)
        ends = count - 1
        head = lax.slice_in_dim(cells, 0, width, axis=dim)
        tail = lax.slice_in_dim(cells, cells.shape[dim] - width, cells.shape[dim], axis=dim)
        cells = jnp.concatenate(
            [
                lax.ppermute(tail, axis, [(i, (i + 1) % count) for i in range(ends)]),
                cells,
                lax.ppermute(head, axis, [((i + 1) % count, i) for i in range(ends)]),
            ],
            axis=dim,
        )
    return cells


def one_axis_at_a_time(x, axes):
    for axis in axes:
        x = lax.psum(x, axis)
    return x


def with_halo(x, sides, width):
    edges = {}
    for axis, dim in sides:
        count, length = (lax.axis_size(axis), x.shape[dim])
        up = [(i, (i + 1) % count) for i in range(count - 1)]
        last = lax.slice_in_dim(x, length - width, length, axis=dim)
        first = lax.slice_in_dim(x, 0, width, axis=dim)
        edges[dim] = (
            lax.ppermute(last, axis, up),
            lax.ppermute(first, axis, [(b, a) for a, b in up]),
        )
    done = []
    for _, dim in sides:
        low, high = edges[dim]
        around = [(width, width) if d in done else (0, 0) for d in range(x.ndim)]
        x = jnp.concatenate([jnp.pad(low, around), x, jnp.pad(high, around)], axis=dim)
        done.append(dim)
    return x


def node_sums(contribs, within, line_index, line_length, count_lines):
    blocks = contribs.shape[0]
    group_size = math.gcd(16, blocks)
    row_count = contribs.shape[1]
    columns = lax.broadcasted_iota(jnp.int32, (1, 1, line_length), 2)
    line_ids = lax.broadcasted_iota(jnp.int32, (1, count_lines), 1)

    def node_add_group(turn_idx, running):
        first_block = turn_idx * group_size
        term_part = lax.dynamic_slice_in_dim(contribs, first_block, group_size, 0)
        node_part = lax.dynamic_slice_in_dim(within, first_block, group_size, 0)
        line_part = lax.dynamic_slice_in_dim(line_index, first_block, group_size, 0)
        one_hot = (node_part[:, :, None] == columns).astype(jnp.float32)
        window = jnp.einsum("bcp,bpn->bcn", term_part, one_hot, precision=highest)
        line_hot = (line_part[:, None] == line_ids).astype(jnp.float32)
        return running + jnp.einsum("bl,bcn->cln", line_hot, window, precision=highest)

    initial = jnp.zeros((row_count, count_lines, line_length), jnp.float32)
    return lax.fori_loop(0, blocks // group_size, node_add_group, initial)


def select_lines(line_hot, field_lines):
    return jnp.einsum("bl,cln->bcn", line_hot, field_lines, precision=highest)


def sweep_terms(
    near_lines, far_lines, within, far_pos, line_index, geometry, live_mask, count_lines
):
    blocks = within.shape[0]
    group_size = math.gcd(16, blocks)
    near_cols = lax.broadcasted_iota(jnp.int32, (1, 1, near_lines.shape[2]), 2)
    far_cols = lax.broadcasted_iota(jnp.int32, (1, 1, far_lines.shape[2]), 2)
    line_ids = lax.broadcasted_iota(jnp.int32, (1, count_lines), 1)

    def sweep_add_group(turn_idx, carry):
        running, energy_sum = carry
        near_hot = (within[:, :, None] == near_cols).astype(jnp.float32)
        far_hot = (far_pos[:, :, None] == far_cols).astype(jnp.float32)
        near_vals = jnp.einsum("bcn,bpn->bcp", near_lines, near_hot, precision=highest)
        far_vals = jnp.einsum("bcn,bpn->bcp", far_lines, far_hot, precision=highest)
        differ = near_vals - far_vals
        gap_value = (
            geometry[:, 0, :] * differ[:, 0, :]
            + geometry[:, 1, :] * differ[:, 1, :]
            + geometry[:, 2, :] * differ[:, 2, :]
            - geometry[:, 3, :]
        )
        depth_value = jnp.where(live_mask, jnp.maximum(-gap_value, 0.0), 0.0)
        contribs = depth_value[:, None, :] * geometry[:, 0:3, :]
        window = jnp.einsum("bcp,bpn->bcn", contribs, near_hot, precision=highest)
        line_hot = (line_index[:, None] == line_ids).astype(jnp.float32)
        running = running + jnp.einsum("bl,bcn->cln", line_hot, window, precision=highest)
        return (running, energy_sum + jnp.sum(depth_value * depth_value))

    initial = (
        jnp.zeros((3, count_lines, near_lines.shape[2]), jnp.float32),
        jnp.zeros((), jnp.float32),
    )
    return lax.fori_loop(0, blocks // group_size, sweep_add_group, initial)


def local(positions, pair_node, pair_line, pair_far, far_line, pair_geom, live_blocks):
    within = pair_node[0, 0, 0]
    line_index = pair_line[0, 0, 0]
    far_pos = pair_far[0, 0, 0]
    far_index = far_line[0, 0, 0]
    geometry = pair_geom[0, 0, 0]
    live_count = live_blocks[0, 0, 0]
    size_x = positions.shape[1]
    size_y = positions.shape[2]
    size_z = positions.shape[3]
    blocks = within.shape[0]
    pair_count = within.shape[1]
    inner_count = blocks // 2
    count_lines = size_x * size_y
    ext_lines = (size_x + 2 * RIM) * (size_y + 2 * RIM)
    ext_z = size_z + 2 * RIM
    devices = lax.axis_size("gx") * lax.axis_size("gy") * lax.axis_size(GZ)
    slot_count = blocks * pair_count
    live_mask = lax.broadcasted_iota(jnp.int32, (blocks, 1), 0) < live_count
    near_hot = (line_index[:, None] == lax.broadcasted_iota(jnp.int32, (1, count_lines), 1)).astype(
        jnp.float32
    )
    far_hot = (far_index[:, None] == lax.broadcasted_iota(jnp.int32, (1, ext_lines), 1)).astype(
        jnp.float32
    )
    live_ones = jnp.broadcast_to(
        jnp.where(live_mask, 1.0, 0.0).astype(jnp.float32), (blocks, pair_count)
    )
    counts = node_sums(live_ones[:, None, :], within, line_index, size_z, count_lines).reshape(
        size_x, size_y, size_z
    )
    widths = ((0, 0), (RIM, RIM), (RIM, RIM), (RIM, RIM))
    padded = extended(positions, (("gx", 1), ("gy", 2), (GZ, 3)), RIM)
    current = positions
    energies = []
    residuals = []
    for sweep_idx in range(SWEEPS):
        near_lines = select_lines(near_hot, current.reshape(3, count_lines, size_z))
        local_pad = jnp.pad(current, widths).reshape(3, ext_lines, ext_z)
        inner_far = select_lines(far_hot[:inner_count], local_pad)
        inner_total, inner_energy = sweep_terms(
            near_lines[:inner_count],
            inner_far,
            within[:inner_count],
            far_pos[:inner_count],
            line_index[:inner_count],
            geometry[:inner_count],
            live_mask[:inner_count],
            count_lines,
        )
        outer_far = select_lines(far_hot[inner_count:], padded.reshape(3, ext_lines, ext_z))
        outer_total, outer_energy = sweep_terms(
            near_lines[inner_count:],
            outer_far,
            within[inner_count:],
            far_pos[inner_count:],
            line_index[inner_count:],
            geometry[inner_count:],
            live_mask[inner_count:],
            count_lines,
        )
        node_total = inner_total + outer_total
        energy_local = inner_energy + outer_energy
        total_energy = one_axis_at_a_time(energy_local, GX_GY_GZ)
        scale_factor = 1.0 / (1.0 + total_energy / (slot_count * devices))
        correction = (
            relax_factor
            * scale_factor
            * node_total.reshape(3, size_x, size_y, size_z)
            / (1.0 + counts)
        )
        current = current + correction
        residual_local = jnp.sum(correction * correction)
        residuals.append(one_axis_at_a_time(residual_local, GX_GY_GZ))
        energies.append(total_energy)
        if sweep_idx + 1 < SWEEPS:
            padded = with_halo(current, (("gx", 1), ("gy", 2), (GZ, 3)), RIM)
    history = jnp.stack(
        [
            jnp.sqrt(1.0 + jnp.stack(energies) / slot_count),
            jnp.sqrt(1.0 + jnp.stack(residuals) / (size_x * size_y * size_z)),
        ]
    )
    return (current, history)


def solution(mesh):
    finer = Mesh(
        mesh.devices.reshape(mesh.shape["gx"], mesh.shape["gy"], 4, 2), ("gx", "gy", "gz_0", "gz_1")
    )
    placed = (
        P(None, "gx", "gy", GZ),
        P("gx", "gy", GZ, None, None),
        P("gx", "gy", GZ, None),
        P("gx", "gy", GZ, None, None),
        P("gx", "gy", GZ, None),
        P("gx", "gy", GZ, None, None, None),
        P("gx", "gy", GZ),
    )
    return jax.shard_map(
        local,
        mesh=finer,
        in_specs=placed,
        out_specs=(P(None, "gx", "gy", GZ), P()),
        check_vma=False,
    )
```

profile of v0, /device:TPU:1, one launch (start us, length us, event | category | flops | bytes accessed | tf_op | source)
XLA Modules:
  0.0 486.6 jit_solution(8755252132308115107)
XLA Ops:
  3.7 5.0 %collective-permute-start = (f32[3,3,16,256]{3,1,2,0:T(4,128)S(1)}, f32[3,3,16,256]{3,1,2,0:T(4,128)S(1)}, u32[]{:S(2)}, u32[]{:S(2)}) collective-permute-start(f32[3,3,16,256]{3,1,2,0:T(4,128)S(1)} %get-tuple-element.628), channel_id=1, source_target_pairs={{0,32},{32,64},{64,96},{1,33},{33,65},{65,97},{2,34},{34,66},{66,9... | collective-permute-start | bytes 442376 | tf_op jit(solution)/shard_map/ppermute | solution.py:24
  12.9 3.0 reshape.413
  23.3 4.2 while.9
  31.2 4.0 collective-permute-start.2
  35.2 2.8 fusion.32
  43.1 4.0 collective-permute-start.5
  48.8 3.2 collective-permute-start.4
  55.0 2.5 pad_maximum_fusion
  66.6 8.1 %psum.280 = f32[]{:T(128)} all-reduce(f32[]{:T(128)S(6)} %add.441), channel_id=1, replica_groups=mesh['gx'=4,'gy'=4,'gz_0'=4,'gz_1'=2] {'gx'}, use_global_device_ids=true, to_apply=%region_2.3 | all-reduce | flops 1 | bytes 8 | tf_op jit(solution)/shard_map/psum | solution.py:35
  75.3 10.6 %psum.281 = f32[]{:T(128)} all-reduce(f32[]{:T(128)} %psum.280), channel_id=1, replica_groups=mesh['gx'=4,'gy'=4,'gz_0'=4,'gz_1'=2] {'gy'}, use_global_device_ids=true, to_apply=%region_3.4 | all-reduce | flops 1 | bytes 8 | tf_op jit(solution)/shard_map/psum | solution.py:35
  86.0 7.8 %psum.282 = f32[]{:T(128)} all-reduce(f32[]{:T(128)} %psum.281), channel_id=1, replica_groups=mesh['gx'=4,'gy'=4,'gz_0'=4,'gz_1'=2] {'gz_0'}, use_global_device_ids=true, to_apply=%region_4.5 | all-reduce | flops 1 | bytes 8 | tf_op jit(solution)/shard_map/psum | solution.py:35
  94.7 11.5 %psum.283 = f32[]{:T(128)} all-reduce(f32[]{:T(128)} %psum.282), channel_id=1, replica_groups=mesh['gx'=4,'gy'=4,'gz_0'=4,'gz_1'=2] {'gz_1'}, use_global_device_ids=true, to_apply=%region_5.6 | all-reduce | flops 1 | bytes 8 | tf_op jit(solution)/shard_map/psum | solution.py:35
  113.6 4.0 collective-permute-start.7
  117.6 3.9 collective-permute-start.6
  125.3 4.4 collective-permute-start.8
  132.3 4.8 select_maximum_fusion.9
  137.1 3.0 reshape.416
  144.9 3.0 reshape.417
  154.2 8.4 %psum.284 = f32[]{:T(128)} all-reduce(f32[]{:T(128)S(6)} %add.451), channel_id=1, replica_groups=mesh['gx'=4,'gy'=4,'gz_0'=4,'gz_1'=2] {'gx'}, use_global_device_ids=true, to_apply=%region_10.11 | all-reduce | flops 1 | bytes 8 | tf_op jit(solution)/shard_map/psum | solution.py:35
  162.5 6.6 %psum.285 = f32[]{:T(128)} all-reduce(f32[]{:T(128)} %psum.284), channel_id=1, replica_groups=mesh['gx'=4,'gy'=4,'gz_0'=4,'gz_1'=2] {'gy'}, use_global_device_ids=true, to_apply=%region_11.12 | all-reduce | flops 1 | bytes 8 | tf_op jit(solution)/shard_map/psum | solution.py:35
  170.8 6.6 %psum.286 = f32[]{:T(128)} all-reduce(f32[]{:T(128)} %psum.285), channel_id=1, replica_groups=mesh['gx'=4,'gy'=4,'gz_0'=4,'gz_1'=2] {'gz_0'}, use_global_device_ids=true, to_apply=%region_12.13 | all-reduce | flops 1 | bytes 8 | tf_op jit(solution)/shard_map/psum | solution.py:35
  178.0 9.3 %psum.287 = f32[]{:T(128)} all-reduce(f32[]{:T(128)} %psum.286), channel_id=1, replica_groups=mesh['gx'=4,'gy'=4,'gz_0'=4,'gz_1'=2] {'gz_1'}, use_global_device_ids=true, to_apply=%region_13.14 | all-reduce | flops 1 | bytes 8 | tf_op jit(solution)/shard_map/psum | solution.py:35
  194.7 4.3 collective-permute-start.13
  198.9 3.6 collective-permute-start.12
  204.3 2.8 fusion.38
  207.1 4.2 collective-permute-start.14
  211.2 2.8 fusion.28
  214.3 4.4 select_maximum_fusion.6
  218.6 3.0 reshape.419
  229.4 2.5 fusion.255
  236.3 8.4 %psum.288 = f32[]{:T(128)} all-reduce(f32[]{:T(128)S(6)} %add.459), channel_id=1, replica_groups=mesh['gx'=4,'gy'=4,'gz_0'=4,'gz_1'=2] {'gx'}, use_global_device_ids=true, to_apply=%region_16.17 | all-reduce | flops 1 | bytes 8 | tf_op jit(solution)/shard_map/psum | solution.py:35
  244.7 8.0 %psum.289 = f32[]{:T(128)} all-reduce(f32[]{:T(128)} %psum.288), channel_id=1, replica_groups=mesh['gx'=4,'gy'=4,'gz_0'=4,'gz_1'=2] {'gy'}, use_global_device_ids=true, to_apply=%region_17.18 | all-reduce | flops 1 | bytes 8 | tf_op jit(solution)/shard_map/psum | solution.py:35
  254.4 8.6 %psum.290 = f32[]{:T(128)} all-reduce(f32[]{:T(128)} %psum.289), channel_id=1, replica_groups=mesh['gx'=4,'gy'=4,'gz_0'=4,'gz_1'=2] {'gz_0'}, use_global_device_ids=true, to_apply=%region_18.19 | all-reduce | flops 1 | bytes 8 | tf_op jit(solution)/shard_map/psum | solution.py:35
  263.5 9.0 %psum.291 = f32[]{:T(128)} all-reduce(f32[]{:T(128)} %psum.290), channel_id=1, replica_groups=mesh['gx'=4,'gy'=4,'gz_0'=4,'gz_1'=2] {'gz_1'}, use_global_device_ids=true, to_apply=%region_19.20 | all-reduce | flops 1 | bytes 8 | tf_op jit(solution)/shard_map/psum | solution.py:35
  280.0 4.0 collective-permute-start.19
  284.0 3.9 collective-permute-start.18
  291.8 4.2 collective-permute-start.20
  298.7 4.8 select_maximum_fusion.3
  303.5 3.0 reshape.422
  311.4 3.0 reshape.423
  320.4 8.4 %psum.292 = f32[]{:T(128)} all-reduce(f32[]{:T(128)S(6)} %add.467), channel_id=1, replica_groups=mesh['gx'=4,'gy'=4,'gz_0'=4,'gz_1'=2] {'gx'}, use_global_device_ids=true, to_apply=%region_22.23 | all-reduce | flops 1 | bytes 8 | tf_op jit(solution)/shard_map/psum | solution.py:35
  328.9 6.5 %psum.293 = f32[]{:T(128)} all-reduce(f32[]{:T(128)} %psum.292), channel_id=1, replica_groups=mesh['gx'=4,'gy'=4,'gz_0'=4,'gz_1'=2] {'gy'}, use_global_device_ids=true, to_apply=%region_23.24 | all-reduce | flops 1 | bytes 8 | tf_op jit(solution)/shard_map/psum | solution.py:35
  337.0 6.6 %psum.294 = f32[]{:T(128)} all-reduce(f32[]{:T(128)} %psum.293), channel_id=1, replica_groups=mesh['gx'=4,'gy'=4,'gz_0'=4,'gz_1'=2] {'gz_0'}, use_global_device_ids=true, to_apply=%region_24.25 | all-reduce | flops 1 | bytes 8 | tf_op jit(solution)/shard_map/psum | solution.py:35
  344.2 9.7 %psum.295 = f32[]{:T(128)} all-reduce(f32[]{:T(128)} %psum.294), channel_id=1, replica_groups=mesh['gx'=4,'gy'=4,'gz_0'=4,'gz_1'=2] {'gz_1'}, use_global_device_ids=true, to_apply=%region_25.26 | all-reduce | flops 1 | bytes 8 | tf_op jit(solution)/shard_map/psum | solution.py:35
  361.3 4.0 collective-permute-start.25
  365.3 3.9 collective-permute-start.24
  370.9 2.8 fusion.34
  373.7 4.2 collective-permute-start.26
  378.0 2.8 fusion.24
  380.8 4.4 select_maximum_fusion
  385.2 3.0 reshape.425
  388.2 2.5 fusion.248
  403.8 2.8 fusion.33
  406.6 8.3 %psum.296 = f32[]{:T(128)} all-reduce(f32[]{:T(128)S(6)} %add.475), channel_id=1, replica_groups=mesh['gx'=4,'gy'=4,'gz_0'=4,'gz_1'=2] {'gx'}, use_global_device_ids=true, to_apply=%region_28.29 | all-reduce | flops 1 | bytes 8 | tf_op jit(solution)/shard_map/psum | solution.py:35
  417.3 7.9 %psum.297 = f32[]{:T(128)} all-reduce(f32[]{:T(128)} %psum.296), channel_id=1, replica_groups=mesh['gx'=4,'gy'=4,'gz_0'=4,'gz_1'=2] {'gy'}, use_global_device_ids=true, to_apply=%region_29.30 | all-reduce | flops 1 | bytes 8 | tf_op jit(solution)/shard_map/psum | solution.py:35
  425.1 8.2 %psum.298 = f32[]{:T(128)} all-reduce(f32[]{:T(128)} %psum.297), channel_id=1, replica_groups=mesh['gx'=4,'gy'=4,'gz_0'=4,'gz_1'=2] {'gz_0'}, use_global_device_ids=true, to_apply=%region_30.31 | all-reduce | flops 1 | bytes 8 | tf_op jit(solution)/shard_map/psum | solution.py:35
  435.6 9.4 %psum.299 = f32[]{:T(128)} all-reduce(f32[]{:T(128)} %psum.298), channel_id=1, replica_groups=mesh['gx'=4,'gy'=4,'gz_0'=4,'gz_1'=2] {'gz_1'}, use_global_device_ids=true, to_apply=%region_31.32 | all-reduce | flops 1 | bytes 8 | tf_op jit(solution)/shard_map/psum | solution.py:35
  445.8 3.1 fusion.96
  449.9 6.8 %all-reduce.23 = (f32[]{:T(128)}, f32[]{:T(128)}, f32[]{:T(128)}, f32[]{:T(128)}, f32[]{:T(128)}) all-reduce(f32[]{:T(128)} %get-tuple-element.530, f32[]{:T(128)} %get-tuple-element.527, f32[]{:T(128)} %get-tuple-element.528, f32[]{:T(128)} %get-tuple-element.529, ...), channel_id=1, replica_groups=mesh['gx'=4,'gy'=4,'gz_0'=4,'gz_1'=2] {'gx'}, use_global_device_ids=true, to_apply=%region_33.34 | all-reduce | flops 5 | bytes 40 | tf_op jit(solution)/shard_map/psum | solution.py:35
  456.7 7.0 %all-reduce.22 = (f32[]{:T(128)}, f32[]{:T(128)}, f32[]{:T(128)}, f32[]{:T(128)}, f32[]{:T(128)}) all-reduce(f32[]{:T(128)} %get-tuple-element.564, f32[]{:T(128)} %get-tuple-element.565, f32[]{:T(128)} %get-tuple-element.566, f32[]{:T(128)} %get-tuple-element.567, ...), channel_id=1, replica_groups=mesh['gx'=4,'gy'=4,'gz_0'=4,'gz_1'=2] {'gy'}, use_global_device_ids=true, to_apply=%region_34.35 | all-reduce | flops 5 | bytes 40 | tf_op jit(solution)/shard_map/psum | solution.py:35
  463.7 6.7 %all-reduce.21 = (f32[]{:T(128)}, f32[]{:T(128)}, f32[]{:T(128)}, f32[]{:T(128)}, f32[]{:T(128)}) all-reduce(f32[]{:T(128)} %get-tuple-element.559, f32[]{:T(128)} %get-tuple-element.560, f32[]{:T(128)} %get-tuple-element.561, f32[]{:T(128)} %get-tuple-element.562, ...), channel_id=1, replica_groups=mesh['gx'=4,'gy'=4,'gz_0'=4,'gz_1'=2] {'gz_0'}, use_global_device_ids=true, to_apply=%region_35.36 | all-reduce | flops 5 | bytes 40 | tf_op jit(solution)/shard_map/psum | solution.py:35
  470.4 8.6 %all-reduce.24 = (f32[1,1]{1,0:T(1,128)}, f32[1,1]{1,0:T(1,128)}, f32[1,1]{1,0:T(1,128)}, f32[1,1]{1,0:T(1,128)}, f32[1,1]{1,0:T(1,128)}) all-reduce(f32[1,1]{1,0:T(1,128)} %bitcast.57, f32[1,1]{1,0:T(1,128)} %bitcast.58, f32[1,1]{1,0:T(1,128)} %bitcast.59, ...), channel_id=1, replica_groups=mesh['gx'=4,'gy'=4,'gz_0'=4,'gz_1'=2] {'gz_1'}, use_global_device_ids=true, to_apply=%region_36.37 | all-reduce | flops 5 | bytes 40 | tf_op jit(solution)/shard_map/psum | solution.py:35
  479.0 3.2 stack.52
  482.2 3.3 stack.46
  (304 shorter events, 138.7 us)
Async XLA Ops:
  0.6 10.2 %copy-start = (f32[3,16,16,256]{3,2,1,0:T(8,128)S(1)}, f32[3,16,16,256]{3,2,1,0:T(8,128)}, u32[]{:S(2)}) copy-start(f32[3,16,16,256]{3,2,1,0:T(8,128)} %param.9) | copy-start | bytes 2359300
  0.6 8.8 %copy-start.21 = (f32[1,1,1,32,4,256]{5,4,3,2,1,0:T(4,128)S(1)}, f32[1,1,1,32,4,256]{5,4,3,2,1,0:T(4,128)}, u32[]{:S(2)}) copy-start(f32[1,1,1,32,4,256]{5,4,3,2,1,0:T(4,128)} %param.14) | copy-start | bytes 393220
  0.6 9.6 %copy-start.30 = (s32[1,1,1,32,256]{4,3,2,1,0:T(8,128)S(1)}, s32[1,1,1,32,256]{4,3,2,1,0:T(8,128)}, u32[]{:S(2)}) copy-start(s32[1,1,1,32,256]{4,3,2,1,0:T(8,128)} %param.12) | copy-start | bytes 98308
  2.4 27.4 %collective-permute-start.1 = (f32[3,3,16,256]{3,1,2,0:T(4,128)S(1)}, f32[3,3,16,256]{3,1,2,0:T(4,128)S(1)}, u32[]{:S(2)}, u32[]{:S(2)}) collective-permute-start(f32[3,3,16,256]{3,1,2,0:T(4,128)S(1)} %get-tuple-element.629), channel_id=1, source_target_pairs={{32,0},{64,32},{96,64},{33,1},{65,33},{97,65},{34,2},{66,34},{98,6... | collective-permute-start | bytes 442376 | tf_op jit(solution)/shard_map/ppermute | solution.py:26
  3.7 26.1 %collective-permute-start = (f32[3,3,16,256]{3,1,2,0:T(4,128)S(1)}, f32[3,3,16,256]{3,1,2,0:T(4,128)S(1)}, u32[]{:S(2)}, u32[]{:S(2)}) collective-permute-start(f32[3,3,16,256]{3,1,2,0:T(4,128)S(1)} %get-tuple-element.628), channel_id=1, source_target_pairs={{0,32},{32,64},{64,96},{1,33},{33,65},{65,97},{2,34},{34,66},{66,9... | collective-permute-start | bytes 442376 | tf_op jit(solution)/shard_map/ppermute | solution.py:24
  9.5 18.1 %copy-start.39 = (s32[16,256]{1,0:T(8,128)}, s32[16,256]{1,0:T(8,128)S(1)}, u32[]{:S(2)}) copy-start(s32[16,256]{1,0:T(8,128)S(1)} %get-tuple-element.650) | copy-start | bytes 49156
  9.5 25.7 %copy-start.36 = (s32[16,256]{1,0:T(8,128)}, s32[16,256]{1,0:T(8,128)S(1)}, u32[]{:S(2)}) copy-start(s32[16,256]{1,0:T(8,128)S(1)} %get-tuple-element.649) | copy-start | bytes 49156
  10.8 8.1 %copy-start.47 = (s32[16,256]{1,0:T(8,128)}, s32[16,256]{1,0:T(8,128)S(1)}, u32[]{:S(2)}) copy-start(s32[16,256]{1,0:T(8,128)S(1)} %get-tuple-element.652) | copy-start | bytes 49156
  16.0 6.6 %copy-start.17 = (pred[32,484]{1,0:T(8,128)(4,1)}, pred[32,484]{1,0:T(8,128)(4,1)S(1)}, u32[]{:S(2)}) copy-start(pred[32,484]{1,0:T(8,128)(4,1)S(1)} %iota_compare_fusion.46) | copy-start | bytes 46468
  16.4 6.5 %copy-start.20 = (s32[1,1,1,32,256]{4,3,2,1,0:T(8,128)S(1)}, s32[1,1,1,32,256]{4,3,2,1,0:T(8,128)}, u32[]{:S(2)}) copy-start(s32[1,1,1,32,256]{4,3,2,1,0:T(8,128)} %param.10) | copy-start | bytes 98308
  29.8 8.2 %copy-start.13 = (f32[3,3,16,256]{3,1,2,0:T(4,128)}, f32[3,3,16,256]{3,1,2,0:T(4,128)S(1)}, u32[]{:S(2)}) copy-start(f32[3,3,16,256]{3,1,2,0:T(4,128)S(1)} %collective-permute-done.1) | copy-start | bytes 442372
  29.8 8.2 %copy-start.14 = (f32[3,3,16,256]{3,1,2,0:T(4,128)}, f32[3,3,16,256]{3,1,2,0:T(4,128)S(1)}, u32[]{:S(2)}) copy-start(f32[3,3,16,256]{3,1,2,0:T(4,128)S(1)} %collective-permute-done) | copy-start | bytes 442372
  29.9 8.1 %collective-permute-start.3 = (f32[3,22,3,256]{3,1,2,0:T(8,128)S(1)}, f32[3,22,3,256]{3,1,2,0:T(8,128)S(1)}, u32[]{:S(2)}, u32[]{:S(2)}) collective-permute-start(f32[3,22,3,256]{3,1,2,0:T(8,128)S(1)} %get-tuple-element.595), channel_id=1, source_target_pairs={{8,0},{16,8},{24,16},{9,1},{17,9},{25,17},{10,2},{18,10},{26,18},{... | collective-permute-start | bytes 608264 | tf_op jit(solution)/shard_map/ppermute | solution.py:26
  31.2 7.5 %collective-permute-start.2 = (f32[3,22,3,256]{3,1,2,0:T(8,128)S(1)}, f32[3,22,3,256]{3,1,2,0:T(8,128)S(1)}, u32[]{:S(2)}, u32[]{:S(2)}) collective-permute-start(f32[3,22,3,256]{3,1,2,0:T(8,128)S(1)} %get-tuple-element.594), channel_id=1, source_target_pairs={{0,8},{8,16},{16,24},{1,9},{9,17},{17,25},{2,10},{10,18},{18,26},{... | collective-permute-start | bytes 608264 | tf_op jit(solution)/shard_map/ppermute | solution.py:24
  43.1 9.6 %collective-permute-start.5 = (f32[3,22,22,3]{2,1,3,0:T(8,128)S(1)}, f32[3,22,22,3]{2,1,3,0:T(8,128)S(1)}, u32[]{:S(2)}, u32[]{:S(2)}) collective-permute-start(f32[3,22,22,3]{2,1,3,0:T(8,128)S(1)} %copy.135), channel_id=1, source_target_pairs={{1,0},{2,1},{3,2},{4,3},{5,4},{6,5},{7,6},{9,8},{10,9},{11,10},{12... | collective-permute-start | bytes 52280 | tf_op jit(solution)/shard_map/ppermute | solution.py:26
  48.8 4.8 collective-permute-start.4
  59.7 6.9 %copy-start.32 = (s32[1,1,1,32]{3,2,1,0:T(1,128)S(1)}, s32[1,1,1,32]{3,2,1,0:T(1,128)}, u32[]{:S(2)}) copy-start(s32[1,1,1,32]{3,2,1,0:T(1,128)} %param.11) | copy-start | bytes 388
  59.7 15.1 %copy-start.29 = (f32[16,3,256]{2,1,0:T(4,128)S(1)}, f32[16,3,256]{2,1,0:T(4,128)}, u32[]{:S(2)}) copy-start(f32[16,3,256]{2,1,0:T(4,128)} %fusion.41) | copy-start | bytes 147460
  62.2 44.7 %copy-start.37 = (s32[16,256]{1,0:T(8,128)S(1)}, s32[16,256]{1,0:T(8,128)}, u32[]{:S(2)}) copy-start(s32[16,256]{1,0:T(8,128)} %copy-done.36) | copy-start | bytes 49156
  66.6 42.4 %copy-start.50 = (s32[16]{0:T(128)}, s32[16]{0:T(128)S(1)}, u32[]{:S(2)}) copy-start(s32[16]{0:T(128)S(1)} %get-tuple-element.655) | copy-start | bytes 196
  66.6 110.7 %copy-start.34 = (s32[16]{0:T(128)}, s32[16]{0:T(128)S(1)}, u32[]{:S(2)}) copy-start(s32[16]{0:T(128)S(1)} %get-tuple-element.656) | copy-start | bytes 196
  109.3 13.9 %copy-start.40 = (s32[16,256]{1,0:T(8,128)S(1)}, s32[16,256]{1,0:T(8,128)}, u32[]{:S(2)}) copy-start(s32[16,256]{1,0:T(8,128)} %copy-done.39) | copy-start | bytes 49156
  110.0 15.3 %collective-permute-start.11 = (f32[3,16,16,3]{3,2,1,0:T(8,128)S(1)}, f32[3,16,16,3]{3,2,1,0:T(8,128)S(1)}, u32[]{:S(2)}, u32[]{:S(2)}) collective-permute-start(f32[3,16,16,3]{3,2,1,0:T(8,128)S(1)} %get-tuple-element.625), channel_id=1, source_target_pairs={{1,0},{2,1},{3,2},{4,3},{5,4},{6,5},{7,6},{9,8},{10,9},{11,10},{12... | collective-permute-start | bytes 27656 | tf_op jit(solution)/shard_map/ppermute | solution.py:48
  112.3 19.6 %collective-permute-start.10 = (f32[3,16,3,256]{3,2,1,0:T(4,128)S(1)}, f32[3,16,3,256]{3,2,1,0:T(4,128)S(1)}, u32[]{:S(2)}, u32[]{:S(2)}) collective-permute-start(f32[3,16,3,256]{3,2,1,0:T(4,128)S(1)} %get-tuple-element.627), channel_id=1, source_target_pairs={{8,0},{16,8},{24,16},{9,1},{17,9},{25,17},{10,2},{18,10},{26,18},{... | collective-permute-start | bytes 442376 | tf_op jit(solution)/shard_map/ppermute | solution.py:48
  113.6 18.4 %collective-permute-start.7 = (f32[3,16,3,256]{3,2,1,0:T(4,128)S(1)}, f32[3,16,3,256]{3,2,1,0:T(4,128)S(1)}, u32[]{:S(2)}, u32[]{:S(2)}) collective-permute-start(f32[3,16,3,256]{3,2,1,0:T(4,128)S(1)} %get-tuple-element.626), channel_id=1, source_target_pairs={{0,8},{8,16},{16,24},{1,9},{9,17},{17,25},{2,10},{10,18},{18,26},{... | collective-permute-start | bytes 442376 | tf_op jit(solution)/shard_map/ppermute | solution.py:47
  117.6 14.3 %collective-permute-start.6 = (f32[3,16,16,3]{3,2,1,0:T(8,128)S(1)}, f32[3,16,16,3]{3,2,1,0:T(8,128)S(1)}, u32[]{:S(2)}, u32[]{:S(2)}) collective-permute-start(f32[3,16,16,3]{3,2,1,0:T(8,128)S(1)} %get-tuple-element.624), channel_id=1, source_target_pairs={{0,1},{1,2},{2,3},{3,4},{4,5},{5,6},{6,7},{8,9},{9,10},{10,11},{11... | collective-permute-start | bytes 27656 | tf_op jit(solution)/shard_map/ppermute | solution.py:47
  121.4 10.5 %collective-permute-start.9 = (f32[3,3,16,256]{3,2,1,0:T(8,128)S(1)}, f32[3,3,16,256]{3,2,1,0:T(8,128)S(1)}, u32[]{:S(2)}, u32[]{:S(2)}) collective-permute-start(f32[3,3,16,256]{3,2,1,0:T(8,128)S(1)} %get-tuple-element.623), channel_id=1, source_target_pairs={{32,0},{64,32},{96,64},{33,1},{65,33},{97,65},{34,2},{66,34},{98,6... | collective-permute-start | bytes 442376 | tf_op jit(solution)/shard_map/ppermute | solution.py:48
  125.3 7.0 %collective-permute-start.8 = (f32[3,3,16,256]{3,2,1,0:T(8,128)S(1)}, f32[3,3,16,256]{3,2,1,0:T(8,128)S(1)}, u32[]{:S(2)}, u32[]{:S(2)}) collective-permute-start(f32[3,3,16,256]{3,2,1,0:T(8,128)S(1)} %get-tuple-element.622), channel_id=1, source_target_pairs={{0,32},{32,64},{64,96},{1,33},{33,65},{65,97},{2,34},{34,66},{66,9... | collective-permute-start | bytes 442376 | tf_op jit(solution)/shard_map/ppermute | solution.py:47
  137.1 5.6 %copy-start.48 = (s32[16,256]{1,0:T(8,128)S(1)}, s32[16,256]{1,0:T(8,128)}, u32[]{:S(2)}) copy-start(s32[16,256]{1,0:T(8,128)} %copy-done.47) | copy-start | bytes 49156
  144.9 5.5 %copy-start.45 = (s32[16,256]{1,0:T(8,128)S(1)}, s32[16,256]{1,0:T(8,128)}, u32[]{:S(2)}) copy-start(s32[16,256]{1,0:T(8,128)} %get-tuple-element.651) | copy-start | bytes 49156
  150.4 39.2 %copy-start.51 = (s32[16]{0:T(128)S(1)}, s32[16]{0:T(128)}, u32[]{:S(2)}) copy-start(s32[16]{0:T(128)} %copy-done.50) | copy-start | bytes 196
  190.4 13.9 %copy-start.41 = (s32[16,256]{1,0:T(8,128)S(1)}, s32[16,256]{1,0:T(8,128)}, u32[]{:S(2)}) copy-start(s32[16,256]{1,0:T(8,128)} %copy-done.39) | copy-start | bytes 49156
  191.1 16.0 %collective-permute-start.17 = (f32[3,16,16,3]{3,2,1,0:T(8,128)S(1)}, f32[3,16,16,3]{3,2,1,0:T(8,128)S(1)}, u32[]{:S(2)}, u32[]{:S(2)}) collective-permute-start(f32[3,16,16,3]{3,2,1,0:T(8,128)S(1)} %get-tuple-element.617), channel_id=1, source_target_pairs={{1,0},{2,1},{3,2},{4,3},{5,4},{6,5},{7,6},{9,8},{10,9},{11,10},{12... | collective-permute-start | bytes 27656 | tf_op jit(solution)/shard_map/ppermute | solution.py:48
  193.4 20.6 %collective-permute-start.16 = (f32[3,16,3,256]{3,2,1,0:T(4,128)S(1)}, f32[3,16,3,256]{3,2,1,0:T(4,128)S(1)}, u32[]{:S(2)}, u32[]{:S(2)}) collective-permute-start(f32[3,16,3,256]{3,2,1,0:T(4,128)S(1)} %get-tuple-element.619), channel_id=1, source_target_pairs={{8,0},{16,8},{24,16},{9,1},{17,9},{25,17},{10,2},{18,10},{26,18},{... | collective-permute-start | bytes 442376 | tf_op jit(solution)/shard_map/ppermute | solution.py:48
  194.7 19.4 %collective-permute-start.13 = (f32[3,16,3,256]{3,2,1,0:T(4,128)S(1)}, f32[3,16,3,256]{3,2,1,0:T(4,128)S(1)}, u32[]{:S(2)}, u32[]{:S(2)}) collective-permute-start(f32[3,16,3,256]{3,2,1,0:T(4,128)S(1)} %get-tuple-element.618), channel_id=1, source_target_pairs={{0,8},{8,16},{16,24},{1,9},{9,17},{17,25},{2,10},{10,18},{18,26},{... | collective-permute-start | bytes 442376 | tf_op jit(solution)/shard_map/ppermute | solution.py:47
  198.9 15.1 %collective-permute-start.12 = (f32[3,16,16,3]{3,2,1,0:T(8,128)S(1)}, f32[3,16,16,3]{3,2,1,0:T(8,128)S(1)}, u32[]{:S(2)}, u32[]{:S(2)}) collective-permute-start(f32[3,16,16,3]{3,2,1,0:T(8,128)S(1)} %get-tuple-element.616), channel_id=1, source_target_pairs={{0,1},{1,2},{2,3},{3,4},{4,5},{5,6},{6,7},{8,9},{9,10},{10,11},{11... | collective-permute-start | bytes 27656 | tf_op jit(solution)/shard_map/ppermute | solution.py:47
  202.5 11.5 %collective-permute-start.15 = (f32[3,3,16,256]{3,2,1,0:T(8,128)S(1)}, f32[3,3,16,256]{3,2,1,0:T(8,128)S(1)}, u32[]{:S(2)}, u32[]{:S(2)}) collective-permute-start(f32[3,3,16,256]{3,2,1,0:T(8,128)S(1)} %get-tuple-element.615), channel_id=1, source_target_pairs={{32,0},{64,32},{96,64},{33,1},{65,33},{97,65},{34,2},{66,34},{98,6... | collective-permute-start | bytes 442376 | tf_op jit(solution)/shard_map/ppermute | solution.py:48
  207.1 7.2 %collective-permute-start.14 = (f32[3,3,16,256]{3,2,1,0:T(8,128)S(1)}, f32[3,3,16,256]{3,2,1,0:T(8,128)S(1)}, u32[]{:S(2)}, u32[]{:S(2)}) collective-permute-start(f32[3,3,16,256]{3,2,1,0:T(8,128)S(1)} %get-tuple-element.614), channel_id=1, source_target_pairs={{0,32},{32,64},{64,96},{1,33},{33,65},{65,97},{2,34},{34,66},{66,9... | collective-permute-start | bytes 442376 | tf_op jit(solution)/shard_map/ppermute | solution.py:47
  229.4 6.8 %copy-start.28 = (f32[16,1,256]{2,0,1:T(8,128)S(1)}, f32[16,1,256]{2,0,1:T(8,128)}, u32[]{:S(2)}) copy-start(f32[16,1,256]{2,0,1:T(8,128)} %get-tuple-element.583) | copy-start | bytes 49156
  229.4 15.4 %copy-start.4 = (f32[16,4,256]{2,0,1:T(8,128)S(1)}, f32[16,4,256]{2,0,1:T(8,128)}, u32[]{:S(2)}) copy-start(f32[16,4,256]{2,0,1:T(8,128)} %copy-done.1) | copy-start | bytes 196612
  229.4 23.4 %copy-start.42 = (s32[16,256]{1,0:T(8,128)S(1)}, s32[16,256]{1,0:T(8,128)}, u32[]{:S(2)}) copy-start(s32[16,256]{1,0:T(8,128)} %copy-done.39) | copy-start | bytes 49156
  229.4 33.6 %copy-start.35 = (s32[16]{0:T(128)S(1)}, s32[16]{0:T(128)}, u32[]{:S(2)}) copy-start(s32[16]{0:T(128)} %copy-done.34) | copy-start | bytes 196
  231.9 41.3 %copy-start.38 = (s32[16,256]{1,0:T(8,128)S(1)}, s32[16,256]{1,0:T(8,128)}, u32[]{:S(2)}) copy-start(s32[16,256]{1,0:T(8,128)} %copy-done.36) | copy-start | bytes 49156
  231.9 42.9 %copy-start.52 = (s32[16]{0:T(128)S(1)}, s32[16]{0:T(128)}, u32[]{:S(2)}) copy-start(s32[16]{0:T(128)} %copy-done.50) | copy-start | bytes 196
  275.4 13.7 %copy-start.33 = (s32[1,1,1,32]{3,2,1,0:T(1,128)S(1)}, s32[1,1,1,32]{3,2,1,0:T(1,128)}, u32[]{:S(2)}) copy-start(s32[1,1,1,32]{3,2,1,0:T(1,128)} %param.11) | copy-start | bytes 388
  275.7 13.9 %copy-start.43 = (s32[16,256]{1,0:T(8,128)S(1)}, s32[16,256]{1,0:T(8,128)}, u32[]{:S(2)}) copy-start(s32[16,256]{1,0:T(8,128)} %copy-done.39) | copy-start | bytes 49156
  276.4 15.3 %collective-permute-start.23 = (f32[3,16,16,3]{3,2,1,0:T(8,128)S(1)}, f32[3,16,16,3]{3,2,1,0:T(8,128)S(1)}, u32[]{:S(2)}, u32[]{:S(2)}) collective-permute-start(f32[3,16,16,3]{3,2,1,0:T(8,128)S(1)} %get-tuple-element.609), channel_id=1, source_target_pairs={{1,0},{2,1},{3,2},{4,3},{5,4},{6,5},{7,6},{9,8},{10,9},{11,10},{12... | collective-permute-start | bytes 27656 | tf_op jit(solution)/shard_map/ppermute | solution.py:48
  278.7 19.5 %collective-permute-start.22 = (f32[3,16,3,256]{3,2,1,0:T(4,128)S(1)}, f32[3,16,3,256]{3,2,1,0:T(4,128)S(1)}, u32[]{:S(2)}, u32[]{:S(2)}) collective-permute-start(f32[3,16,3,256]{3,2,1,0:T(4,128)S(1)} %get-tuple-element.611), channel_id=1, source_target_pairs={{8,0},{16,8},{24,16},{9,1},{17,9},{25,17},{10,2},{18,10},{26,18},{... | collective-permute-start | bytes 442376 | tf_op jit(solution)/shard_map/ppermute | solution.py:48
  280.0 18.2 %collective-permute-start.19 = (f32[3,16,3,256]{3,2,1,0:T(4,128)S(1)}, f32[3,16,3,256]{3,2,1,0:T(4,128)S(1)}, u32[]{:S(2)}, u32[]{:S(2)}) collective-permute-start(f32[3,16,3,256]{3,2,1,0:T(4,128)S(1)} %get-tuple-element.610), channel_id=1, source_target_pairs={{0,8},{8,16},{16,24},{1,9},{9,17},{17,25},{2,10},{10,18},{18,26},{... | collective-permute-start | bytes 442376 | tf_op jit(solution)/shard_map/ppermute | solution.py:47
  284.0 14.1 %collective-permute-start.18 = (f32[3,16,16,3]{3,2,1,0:T(8,128)S(1)}, f32[3,16,16,3]{3,2,1,0:T(8,128)S(1)}, u32[]{:S(2)}, u32[]{:S(2)}) collective-permute-start(f32[3,16,16,3]{3,2,1,0:T(8,128)S(1)} %get-tuple-element.608), channel_id=1, source_target_pairs={{0,1},{1,2},{2,3},{3,4},{4,5},{5,6},{6,7},{8,9},{9,10},{10,11},{11... | collective-permute-start | bytes 27656 | tf_op jit(solution)/shard_map/ppermute | solution.py:47
  287.9 10.3 %collective-permute-start.21 = (f32[3,3,16,256]{3,2,1,0:T(8,128)S(1)}, f32[3,3,16,256]{3,2,1,0:T(8,128)S(1)}, u32[]{:S(2)}, u32[]{:S(2)}) collective-permute-start(f32[3,3,16,256]{3,2,1,0:T(8,128)S(1)} %get-tuple-element.607), channel_id=1, source_target_pairs={{32,0},{64,32},{96,64},{33,1},{65,33},{97,65},{34,2},{66,34},{98,6... | collective-permute-start | bytes 442376 | tf_op jit(solution)/shard_map/ppermute | solution.py:48
  291.8 7.0 %collective-permute-start.20 = (f32[3,3,16,256]{3,2,1,0:T(8,128)S(1)}, f32[3,3,16,256]{3,2,1,0:T(8,128)S(1)}, u32[]{:S(2)}, u32[]{:S(2)}) collective-permute-start(f32[3,3,16,256]{3,2,1,0:T(8,128)S(1)} %get-tuple-element.606), channel_id=1, source_target_pairs={{0,32},{32,64},{64,96},{1,33},{33,65},{65,97},{2,34},{34,66},{66,9... | collective-permute-start | bytes 442376 | tf_op jit(solution)/shard_map/ppermute | solution.py:47
  303.5 5.5 %copy-start.49 = (s32[16,256]{1,0:T(8,128)S(1)}, s32[16,256]{1,0:T(8,128)}, u32[]{:S(2)}) copy-start(s32[16,256]{1,0:T(8,128)} %copy-done.47) | copy-start | bytes 49156
  357.0 13.9 %copy-start.44 = (s32[16,256]{1,0:T(8,128)S(1)}, s32[16,256]{1,0:T(8,128)}, u32[]{:S(2)}) copy-start(s32[16,256]{1,0:T(8,128)} %copy-done.39) | copy-start | bytes 49156
  357.8 16.0 %collective-permute-start.29 = (f32[3,16,16,3]{3,2,1,0:T(8,128)S(1)}, f32[3,16,16,3]{3,2,1,0:T(8,128)S(1)}, u32[]{:S(2)}, u32[]{:S(2)}) collective-permute-start(f32[3,16,16,3]{3,2,1,0:T(8,128)S(1)} %get-tuple-element.601), channel_id=1, source_target_pairs={{1,0},{2,1},{3,2},{4,3},{5,4},{6,5},{7,6},{9,8},{10,9},{11,10},{12... | collective-permute-start | bytes 27656 | tf_op jit(solution)/shard_map/ppermute | solution.py:48
  360.0 20.7 %collective-permute-start.28 = (f32[3,16,3,256]{3,2,1,0:T(4,128)S(1)}, f32[3,16,3,256]{3,2,1,0:T(4,128)S(1)}, u32[]{:S(2)}, u32[]{:S(2)}) collective-permute-start(f32[3,16,3,256]{3,2,1,0:T(4,128)S(1)} %get-tuple-element.603), channel_id=1, source_target_pairs={{8,0},{16,8},{24,16},{9,1},{17,9},{25,17},{10,2},{18,10},{26,18},{... | collective-permute-start | bytes 442376 | tf_op jit(solution)/shard_map/ppermute | solution.py:48
  361.3 19.4 %collective-permute-start.25 = (f32[3,16,3,256]{3,2,1,0:T(4,128)S(1)}, f32[3,16,3,256]{3,2,1,0:T(4,128)S(1)}, u32[]{:S(2)}, u32[]{:S(2)}) collective-permute-start(f32[3,16,3,256]{3,2,1,0:T(4,128)S(1)} %get-tuple-element.602), channel_id=1, source_target_pairs={{0,8},{8,16},{16,24},{1,9},{9,17},{17,25},{2,10},{10,18},{18,26},{... | collective-permute-start | bytes 442376 | tf_op jit(solution)/shard_map/ppermute | solution.py:47
  365.3 15.4 %collective-permute-start.24 = (f32[3,16,16,3]{3,2,1,0:T(8,128)S(1)}, f32[3,16,16,3]{3,2,1,0:T(8,128)S(1)}, u32[]{:S(2)}, u32[]{:S(2)}) collective-permute-start(f32[3,16,16,3]{3,2,1,0:T(8,128)S(1)} %get-tuple-element.600), channel_id=1, source_target_pairs={{0,1},{1,2},{2,3},{3,4},{4,5},{5,6},{6,7},{8,9},{9,10},{10,11},{11... | collective-permute-start | bytes 27656 | tf_op jit(solution)/shard_map/ppermute | solution.py:47
  369.2 11.6 %collective-permute-start.27 = (f32[3,3,16,256]{3,2,1,0:T(8,128)S(1)}, f32[3,3,16,256]{3,2,1,0:T(8,128)S(1)}, u32[]{:S(2)}, u32[]{:S(2)}) collective-permute-start(f32[3,3,16,256]{3,2,1,0:T(8,128)S(1)} %get-tuple-element.599), channel_id=1, source_target_pairs={{32,0},{64,32},{96,64},{33,1},{65,33},{97,65},{34,2},{66,34},{98,6... | collective-permute-start | bytes 442376 | tf_op jit(solution)/shard_map/ppermute | solution.py:48
  373.7 7.0 %collective-permute-start.26 = (f32[3,3,16,256]{3,2,1,0:T(8,128)S(1)}, f32[3,3,16,256]{3,2,1,0:T(8,128)S(1)}, u32[]{:S(2)}, u32[]{:S(2)}) collective-permute-start(f32[3,3,16,256]{3,2,1,0:T(8,128)S(1)} %get-tuple-element.598), channel_id=1, source_target_pairs={{0,32},{32,64},{64,96},{1,33},{33,65},{65,97},{2,34},{34,66},{66,9... | collective-permute-start | bytes 442376 | tf_op jit(solution)/shard_map/ppermute | solution.py:47
  398.5 47.3 %copy-start.7 = (f32[3,256,256]{1,2,0:T(8,128)S(1)}, f32[3,256,256]{1,2,0:T(8,128)}, u32[]{:S(2)}) copy-start(f32[3,256,256]{1,2,0:T(8,128)} %copy-done.6) | copy-start | bytes 2359300
  398.5 47.3 %copy-start.9 = (f32[3,256,256]{1,2,0:T(8,128)S(1)}, f32[3,256,256]{1,2,0:T(8,128)}, u32[]{:S(2)}) copy-start(f32[3,256,256]{1,2,0:T(8,128)} %copy-done.8) | copy-start | bytes 2359300
  398.5 47.3 %copy-start.11 = (f32[3,256,256]{1,2,0:T(8,128)S(1)}, f32[3,256,256]{1,2,0:T(8,128)}, u32[]{:S(2)}) copy-start(f32[3,256,256]{1,2,0:T(8,128)} %copy-done.10) | copy-start | bytes 2359300
  400.9 44.9 %copy-start.53 = (s32[16]{0:T(128)S(1)}, s32[16]{0:T(128)}, u32[]{:S(2)}) copy-start(s32[16]{0:T(128)} %copy-done.50) | copy-start | bytes 196
  (21 other events, 71.3 us)
where the time goes:
time: 496 us; the launch traced here: 487 us
  blocking collectives  197 us (40%)
  matrix products  104 us (21%)
  starting transfers between devices  86.6 us (17%)
  local copies, waits for them, and re-layouts  48.9 us (10%)
  other arithmetic  35.3 us (7%)
  between operations  12.6 us (3%)
    psum x24, blocking collectives, one_axis_at_a_time(): x = lax.psum(x, axis)  197 us
    ppermute x12, starting transfers between devices, with_halo(): lax.ppermute(last, axis, up)  48.5 us
    dot_general x15, matrix products, select_lines(): return jnp.einsum('bl,cln->bcn', line_hot, field_lines, precision=highest)  27.1 us
    dot_general x10, matrix products, sweep_add_group(): jnp.einsum('bcn,bpn->bcp', near_lines, near_hot, precision=highest)  24.6 us
    ppermute x12, starting transfers between devices, with_halo(): lax.ppermute(first, axis, [(b, a) for a, b in up])  19.3 us
    dot_general x10, matrix products, sweep_add_group(): far_vals = jnp.einsum('bcn,bpn->bcp', far_lines, far_hot, precision=highest)  19.3 us
    dot_general x10, matrix products, sweep_add_group(): window = jnp.einsum('bcp,bpn->bcn', contribs, near_hot, precision=highest)  18.6 us
    concatenate x4, other arithmetic, with_halo(): jnp.concatenate([jnp.pad(low, around), x, jnp.pad(high, around)], axis=dim)  18.4 us
  transfers between devices with their start and end apart: 30, of which 5 were waited for; matrix products, arithmetic and copies ran while one was open for 10% of the time, Pallas kernels for 0%

commit v1 on v0

--- a/solution.py
+++ b/solution.py
@@ -32,7 +32,7 @@
 
 def one_axis_at_a_time(x, axes):
     for axis in axes:
-        x = lax.psum(x, axis)
+        x = jnp.sum(lax.all_gather(x, axis), axis=0)
     return x
 
 

time: 496 us -> 561 us (1.13)
  local copies, waits for them, and re-layouts: 48.9 us -> 101 us
  other arithmetic: 35.3 us -> 60.6 us
  blocking collectives: 197 us -> 182 us
    psum x24 -> x0, blocking collectives: 197 us -> none  [one_axis_at_a_time(): x = lax.psum(x, axis)]
    unnamed x0 -> x24, blocking collectives: none -> 182 us
    unnamed x113 -> x223, local copies, waits for them, and re-layouts: 3.97 us -> 56.2 us
    reduce_sum x0 -> x40, other arithmetic: none -> 24.2 us  [one_axis_at_a_time(): x = jnp.sum(lax.all_gather(x, axis), axis=0)]
  transfers between devices with their start and end apart: 30 -> 30, of which waited for: 5 -> 5; matrix products, arithmetic and copies ran while one was open for 10% -> 9% of each run, Pallas kernels for 0% -> 0%
where the time goes in v1:
time: 561 us; the launch traced here: 551 us
  blocking collectives  182 us (32%)
  matrix products  106 us (19%)
  local copies, waits for them, and re-layouts  101 us (18%)
  starting transfers between devices  86.2 us (15%)
  other arithmetic  60.6 us (11%)
  between operations  12.6 us (2%)
    unnamed x24, blocking collectives  182 us
    unnamed x223, local copies, waits for them, and re-layouts  56.2 us
    ppermute x12, starting transfers between devices, with_halo(): lax.ppermute(last, axis, up)  47.6 us
    dot_general x15, matrix products, select_lines(): return jnp.einsum('bl,cln->bcn', line_hot, field_lines, precision=highest)  27.2 us
    dot_general x10, matrix products, sweep_add_group(): jnp.einsum('bcn,bpn->bcp', near_lines, near_hot, precision=highest)  25.2 us
    reduce_sum x40, other arithmetic, one_axis_at_a_time(): x = jnp.sum(lax.all_gather(x, axis), axis=0)  24.2 us
    ppermute x12, starting transfers between devices, with_halo(): lax.ppermute(first, axis, [(b, a) for a, b in up])  19.6 us
    dot_general x10, matrix products, sweep_add_group(): far_vals = jnp.einsum('bcn,bpn->bcp', far_lines, far_hot, precision=highest)  19.3 us
  transfers between devices with their start and end apart: 30, of which 5 were waited for; matrix products, arithmetic and copies ran while one was open for 9% of the time, Pallas kernels for 0%

profile of v1, /device:TPU:1, one launch (start us, length us, event | category | flops | bytes accessed | tf_op | source)
XLA Modules:
  0.0 551.0 jit_solution(2219014813112868592)
XLA Ops:
  3.7 5.0 collective-permute-start
  12.9 3.0 reshape.413
  25.1 4.3 while.9
  33.1 4.0 collective-permute-start.2
  37.2 2.8 fusion.32
  45.1 4.0 collective-permute-start.5
  50.8 3.5 collective-permute-start.4
  57.6 2.5 pad_maximum_fusion
  62.3 2.6 fusion.257
  70.8 7.6 %all-reduce.21 = f32[4]{0:T(128)S(1)} all-reduce(f32[4]{0:T(128)S(1)} %dynamic-update-slice), channel_id=1, replica_groups=mesh['gx'=4,'gy'=4,'gz_0'=4,'gz_1'=2] {'gx'}, use_global_device_ids=true, to_apply=%add.21 | all-reduce | flops 4 | bytes 32
  81.0 9.9 %all-reduce.22 = f32[4]{0:T(128)S(1)} all-reduce(f32[4]{0:T(128)S(1)} %dynamic-update-slice.1), channel_id=1, replica_groups=mesh['gx'=4,'gy'=4,'gz_0'=4,'gz_1'=2] {'gy'}, use_global_device_ids=true, to_apply=%add.22 | all-reduce | flops 4 | bytes 32
  93.4 7.3 %all-reduce.23 = f32[4]{0:T(128)S(1)} all-reduce(f32[4]{0:T(128)S(1)} %dynamic-update-slice.2), channel_id=1, replica_groups=mesh['gx'=4,'gy'=4,'gz_0'=4,'gz_1'=2] {'gz_0'}, use_global_device_ids=true, to_apply=%add.23 | all-reduce | flops 4 | bytes 32
  102.7 10.2 %all-reduce.24 = f32[2]{0:T(128)S(1)} all-reduce(f32[2]{0:T(128)S(1)} %dynamic-update-slice.3), channel_id=1, replica_groups=mesh['gx'=4,'gy'=4,'gz_0'=4,'gz_1'=2] {'gz_1'}, use_global_device_ids=true, to_apply=%add.24 | all-reduce | flops 2 | bytes 16
  120.8 4.0 collective-permute-start.7
  124.8 3.9 collective-permute-start.6
  132.6 4.2 collective-permute-start.8
  139.6 4.8 select_maximum_fusion.9
  144.4 3.0 reshape.416
  152.2 3.0 reshape.417
  162.2 7.9 %all-reduce.25 = f32[4]{0:T(128)S(1)} all-reduce(f32[4]{0:T(128)S(1)} %dynamic-update-slice.4), channel_id=1, replica_groups=mesh['gx'=4,'gy'=4,'gz_0'=4,'gz_1'=2] {'gx'}, use_global_device_ids=true, to_apply=%add.25 | all-reduce | flops 4 | bytes 32
  172.2 6.0 %all-reduce.26 = f32[4]{0:T(128)S(1)} all-reduce(f32[4]{0:T(128)S(1)} %dynamic-update-slice.5), channel_id=1, replica_groups=mesh['gx'=4,'gy'=4,'gz_0'=4,'gz_1'=2] {'gy'}, use_global_device_ids=true, to_apply=%add.26 | all-reduce | flops 4 | bytes 32
  181.7 6.0 %all-reduce.27 = f32[4]{0:T(128)S(1)} all-reduce(f32[4]{0:T(128)S(1)} %dynamic-update-slice.6), channel_id=1, replica_groups=mesh['gx'=4,'gy'=4,'gz_0'=4,'gz_1'=2] {'gz_0'}, use_global_device_ids=true, to_apply=%add.27 | all-reduce | flops 4 | bytes 32
  190.2 8.6 %all-reduce.28 = f32[2]{0:T(128)S(1)} all-reduce(f32[2]{0:T(128)S(1)} %dynamic-update-slice.7), channel_id=1, replica_groups=mesh['gx'=4,'gy'=4,'gz_0'=4,'gz_1'=2] {'gz_1'}, use_global_device_ids=true, to_apply=%add.28 | all-reduce | flops 2 | bytes 16
  207.0 4.3 collective-permute-start.13
  211.3 3.6 collective-permute-start.12
  216.8 2.8 fusion.38
  219.6 4.0 collective-permute-start.14
  223.6 2.8 fusion.28
  226.8 4.4 select_maximum_fusion.6
  231.2 3.0 reshape.419
  249.5 7.9 %all-reduce.29 = f32[4]{0:T(128)S(1)} all-reduce(f32[4]{0:T(128)S(1)} %dynamic-update-slice.8), channel_id=1, replica_groups=mesh['gx'=4,'gy'=4,'gz_0'=4,'gz_1'=2] {'gx'}, use_global_device_ids=true, to_apply=%add.29 | all-reduce | flops 4 | bytes 32
  259.5 7.4 %all-reduce.30 = f32[4]{0:T(128)S(1)} all-reduce(f32[4]{0:T(128)S(1)} %dynamic-update-slice.9), channel_id=1, replica_groups=mesh['gx'=4,'gy'=4,'gz_0'=4,'gz_1'=2] {'gy'}, use_global_device_ids=true, to_apply=%add.30 | all-reduce | flops 4 | bytes 32
  270.4 7.9 %all-reduce.31 = f32[4]{0:T(128)S(1)} all-reduce(f32[4]{0:T(128)S(1)} %dynamic-update-slice.10), channel_id=1, replica_groups=mesh['gx'=4,'gy'=4,'gz_0'=4,'gz_1'=2] {'gz_0'}, use_global_device_ids=true, to_apply=%add.31 | all-reduce | flops 4 | bytes 32
  280.9 8.8 %all-reduce.32 = f32[2]{0:T(128)S(1)} all-reduce(f32[2]{0:T(128)S(1)} %dynamic-update-slice.11), channel_id=1, replica_groups=mesh['gx'=4,'gy'=4,'gz_0'=4,'gz_1'=2] {'gz_1'}, use_global_device_ids=true, to_apply=%add.32 | all-reduce | flops 2 | bytes 16
  297.8 4.0 collective-permute-start.19
  301.8 3.9 collective-permute-start.18
  307.4 2.8 fusion.36
  310.2 4.0 collective-permute-start.20
  317.1 4.8 select_maximum_fusion.3
  321.9 3.0 reshape.422
  329.8 3.0 reshape.423
  339.6 7.9 %all-reduce.33 = f32[4]{0:T(128)S(1)} all-reduce(f32[4]{0:T(128)S(1)} %dynamic-update-slice.12), channel_id=1, replica_groups=mesh['gx'=4,'gy'=4,'gz_0'=4,'gz_1'=2] {'gx'}, use_global_device_ids=true, to_apply=%add.33 | all-reduce | flops 4 | bytes 32
  349.7 6.0 %all-reduce.34 = f32[4]{0:T(128)S(1)} all-reduce(f32[4]{0:T(128)S(1)} %dynamic-update-slice.13), channel_id=1, replica_groups=mesh['gx'=4,'gy'=4,'gz_0'=4,'gz_1'=2] {'gy'}, use_global_device_ids=true, to_apply=%add.34 | all-reduce | flops 4 | bytes 32
  359.3 6.2 %all-reduce.35 = f32[4]{0:T(128)S(1)} all-reduce(f32[4]{0:T(128)S(1)} %dynamic-update-slice.14), channel_id=1, replica_groups=mesh['gx'=4,'gy'=4,'gz_0'=4,'gz_1'=2] {'gz_0'}, use_global_device_ids=true, to_apply=%add.35 | all-reduce | flops 4 | bytes 32
  368.2 9.2 %all-reduce.36 = f32[2]{0:T(128)S(1)} all-reduce(f32[2]{0:T(128)S(1)} %dynamic-update-slice.15), channel_id=1, replica_groups=mesh['gx'=4,'gy'=4,'gz_0'=4,'gz_1'=2] {'gz_1'}, use_global_device_ids=true, to_apply=%add.36 | all-reduce | flops 2 | bytes 16
  385.5 4.0 collective-permute-start.25
  389.5 3.9 collective-permute-start.24
  395.1 2.8 fusion.34
  397.9 4.0 collective-permute-start.26
  401.9 2.8 fusion.24
  404.8 4.4 select_maximum_fusion
  409.2 3.0 reshape.425
  428.4 2.8 fusion.33
  431.3 7.9 %all-reduce.37 = f32[4]{0:T(128)S(1)} all-reduce(f32[4]{0:T(128)S(1)} %dynamic-update-slice.16), channel_id=1, replica_groups=mesh['gx'=4,'gy'=4,'gz_0'=4,'gz_1'=2] {'gx'}, use_global_device_ids=true, to_apply=%add.37 | all-reduce | flops 4 | bytes 32
  443.4 7.1 %all-reduce.38 = f32[4]{0:T(128)S(1)} all-reduce(f32[4]{0:T(128)S(1)} %dynamic-update-slice.17), channel_id=1, replica_groups=mesh['gx'=4,'gy'=4,'gz_0'=4,'gz_1'=2] {'gy'}, use_global_device_ids=true, to_apply=%add.38 | all-reduce | flops 4 | bytes 32
  452.4 7.6 %all-reduce.39 = f32[4]{0:T(128)S(1)} all-reduce(f32[4]{0:T(128)S(1)} %dynamic-update-slice.18), channel_id=1, replica_groups=mesh['gx'=4,'gy'=4,'gz_0'=4,'gz_1'=2] {'gz_0'}, use_global_device_ids=true, to_apply=%add.39 | all-reduce | flops 4 | bytes 32
  464.2 8.7 %all-reduce.40 = f32[2]{0:T(128)S(1)} all-reduce(f32[2]{0:T(128)S(1)} %dynamic-update-slice.19), channel_id=1, replica_groups=mesh['gx'=4,'gy'=4,'gz_0'=4,'gz_1'=2] {'gz_1'}, use_global_device_ids=true, to_apply=%add.40 | all-reduce | flops 2 | bytes 16
  474.2 3.8 fusion.96
  484.6 6.1 %all-reduce.63 = (f32[4]{0:T(128)S(1)}, f32[4]{0:T(128)S(1)}, f32[4]{0:T(128)S(1)}, f32[4]{0:T(128)S(1)}, f32[4]{0:T(128)S(1)}) all-reduce(f32[4]{0:T(128)S(1)} %dynamic-update-slice.20, f32[4]{0:T(128)S(1)} %dynamic-update-slice.24, f32[4]{0:T(128)S(1)} %dynamic-update-slice.28, ...), channel_id=1, replica_groups=mesh['gx'=4,'gy'=4,'gz_0'=4,'gz_1'=2] {'gx'}, use_global_device_ids=true, to_apply=%add.41 | all-reduce | flops 20 | bytes 160
  500.4 6.3 %all-reduce.62 = (f32[4]{0:T(128)S(1)}, f32[4]{0:T(128)S(1)}, f32[4]{0:T(128)S(1)}, f32[4]{0:T(128)S(1)}, f32[4]{0:T(128)S(1)}) all-reduce(f32[4]{0:T(128)S(1)} %dynamic-update-slice.21, f32[4]{0:T(128)S(1)} %dynamic-update-slice.25, f32[4]{0:T(128)S(1)} %dynamic-update-slice.29, ...), channel_id=1, replica_groups=mesh['gx'=4,'gy'=4,'gz_0'=4,'gz_1'=2] {'gy'}, use_global_device_ids=true, to_apply=%add.42 | all-reduce | flops 20 | bytes 160
  515.7 6.0 %all-reduce.61 = (f32[4]{0:T(128)S(1)}, f32[4]{0:T(128)S(1)}, f32[4]{0:T(128)S(1)}, f32[4]{0:T(128)S(1)}, f32[4]{0:T(128)S(1)}) all-reduce(f32[4]{0:T(128)S(1)} %dynamic-update-slice.22, f32[4]{0:T(128)S(1)} %dynamic-update-slice.26, f32[4]{0:T(128)S(1)} %dynamic-update-slice.30, ...), channel_id=1, replica_groups=mesh['gx'=4,'gy'=4,'gz_0'=4,'gz_1'=2] {'gz_0'}, use_global_device_ids=true, to_apply=%add.43 | all-reduce | flops 20 | bytes 160
  533.0 7.9 %all-reduce.64 = (f32[2]{0:T(128)S(1)}, f32[2]{0:T(128)S(1)}, f32[2]{0:T(128)S(1)}, f32[2]{0:T(128)S(1)}, f32[2]{0:T(128)S(1)}) all-reduce(f32[2]{0:T(128)S(1)} %dynamic-update-slice.23, f32[2]{0:T(128)S(1)} %dynamic-update-slice.27, f32[2]{0:T(128)S(1)} %dynamic-update-slice.31, ...), channel_id=1, replica_groups=mesh['gx'=4,'gy'=4,'gz_0'=4,'gz_1'=2] {'gz_1'}, use_global_device_ids=true, to_apply=%add.44 | all-reduce | flops 10 | bytes 80
  543.9 3.0 stack.52
  546.9 3.4 stack.46
  (454 shorter events, 218.2 us)
Async XLA Ops:
  0.6 10.2 %copy-start = (f32[3,16,16,256]{3,2,1,0:T(8,128)S(1)}, f32[3,16,16,256]{3,2,1,0:T(8,128)}, u32[]{:S(2)}) copy-start(f32[3,16,16,256]{3,2,1,0:T(8,128)} %param.9) | copy-start | bytes 2359300
  2.4 29.3 %collective-permute-start.1 = (f32[3,3,16,256]{3,1,2,0:T(4,128)S(1)}, f32[3,3,16,256]{3,1,2,0:T(4,128)S(1)}, u32[]{:S(2)}, u32[]{:S(2)}) collective-permute-start(f32[3,3,16,256]{3,1,2,0:T(4,128)S(1)} %get-tuple-element.629), channel_id=1, source_target_pairs={{32,0},{64,32},{96,64},{33,1},{65,33},{97,65},{34,2},{66,34},{98,6... | collective-permute-start | bytes 442376 | tf_op jit(solution)/shard_map/ppermute | solution.py:26
  3.7 28.0 %collective-permute-start = (f32[3,3,16,256]{3,1,2,0:T(4,128)S(1)}, f32[3,3,16,256]{3,1,2,0:T(4,128)S(1)}, u32[]{:S(2)}, u32[]{:S(2)}) collective-permute-start(f32[3,3,16,256]{3,1,2,0:T(4,128)S(1)} %get-tuple-element.628), channel_id=1, source_target_pairs={{0,32},{32,64},{64,96},{1,33},{33,65},{65,97},{2,34},{34,66},{66,9... | collective-permute-start | bytes 442376 | tf_op jit(solution)/shard_map/ppermute | solution.py:24
  9.5 13.9 %copy-start.45 = (s32[16,256]{1,0:T(8,128)}, s32[16,256]{1,0:T(8,128)S(1)}, u32[]{:S(2)}) copy-start(s32[16,256]{1,0:T(8,128)S(1)} %get-tuple-element.650) | copy-start | bytes 49156
  9.5 27.7 %copy-start.38 = (s32[16,256]{1,0:T(8,128)}, s32[16,256]{1,0:T(8,128)S(1)}, u32[]{:S(2)}) copy-start(s32[16,256]{1,0:T(8,128)S(1)} %get-tuple-element.649) | copy-start | bytes 49156
  16.5 13.0 %copy-start.35 = (s32[16]{0:T(128)}, s32[16]{0:T(128)S(1)}, u32[]{:S(2)}) copy-start(s32[16]{0:T(128)S(1)} %get-tuple-element.656) | copy-start | bytes 196
  31.8 8.1 %collective-permute-start.3 = (f32[3,22,3,256]{3,1,2,0:T(8,128)S(1)}, f32[3,22,3,256]{3,1,2,0:T(8,128)S(1)}, u32[]{:S(2)}, u32[]{:S(2)}) collective-permute-start(f32[3,22,3,256]{3,1,2,0:T(8,128)S(1)} %get-tuple-element.595), channel_id=1, source_target_pairs={{8,0},{16,8},{24,16},{9,1},{17,9},{25,17},{10,2},{18,10},{26,18},{... | collective-permute-start | bytes 608264 | tf_op jit(solution)/shard_map/ppermute | solution.py:26
  33.1 7.5 %collective-permute-start.2 = (f32[3,22,3,256]{3,1,2,0:T(8,128)S(1)}, f32[3,22,3,256]{3,1,2,0:T(8,128)S(1)}, u32[]{:S(2)}, u32[]{:S(2)}) collective-permute-start(f32[3,22,3,256]{3,1,2,0:T(8,128)S(1)} %get-tuple-element.594), channel_id=1, source_target_pairs={{0,8},{8,16},{16,24},{1,9},{9,17},{17,25},{2,10},{10,18},{18,26},{... | collective-permute-start | bytes 608264 | tf_op jit(solution)/shard_map/ppermute | solution.py:24
  42.0 13.0 %copy-start.67 = (u32[128]{0:T(128)S(1)}, u32[128]{0:T(128)}, u32[]{:S(2)}) copy-start(u32[128]{0:T(128)} %constant.164) | copy-start | bytes 1540
  45.1 10.4 %collective-permute-start.5 = (f32[3,22,22,3]{2,1,3,0:T(8,128)S(1)}, f32[3,22,22,3]{2,1,3,0:T(8,128)S(1)}, u32[]{:S(2)}, u32[]{:S(2)}) collective-permute-start(f32[3,22,22,3]{2,1,3,0:T(8,128)S(1)} %copy.135), channel_id=1, source_target_pairs={{1,0},{2,1},{3,2},{4,3},{5,4},{6,5},{7,6},{9,8},{10,9},{11,10},{12... | collective-permute-start | bytes 52280 | tf_op jit(solution)/shard_map/ppermute | solution.py:26
  50.8 5.4 collective-permute-start.4
  62.3 18.1 %copy-start.65 = (u32[128]{0:T(128)S(1)}, u32[128]{0:T(128)}, u32[]{:S(2)}) copy-start(u32[128]{0:T(128)} %constant.174) | copy-start | bytes 1540
  62.3 30.6 %copy-start.64 = (u32[128]{0:T(128)S(1)}, u32[128]{0:T(128)}, u32[]{:S(2)}) copy-start(u32[128]{0:T(128)} %constant.179) | copy-start | bytes 1540
  62.3 51.9 %copy-start.39 = (s32[16,256]{1,0:T(8,128)S(1)}, s32[16,256]{1,0:T(8,128)}, u32[]{:S(2)}) copy-start(s32[16,256]{1,0:T(8,128)} %copy-done.38) | copy-start | bytes 49156
  62.3 53.5 %copy-start.13 = (f32[3,256,256]{1,2,0:T(8,128)S(1)}, f32[3,256,256]{1,2,0:T(8,128)}, u32[]{:S(2)}) copy-start(f32[3,256,256]{1,2,0:T(8,128)} %fusion.140) | copy-start | bytes 2359300
  62.3 53.5 %copy-start.58 = (s32[16]{0:T(128)S(1)}, s32[16]{0:T(128)}, u32[]{:S(2)}) copy-start(s32[16]{0:T(128)} %get-tuple-element.655) | copy-start | bytes 196
  116.4 13.6 %copy-start.33 = (s32[1,1,1,32]{3,2,1,0:T(1,128)S(1)}, s32[1,1,1,32]{3,2,1,0:T(1,128)}, u32[]{:S(2)}) copy-start(s32[1,1,1,32]{3,2,1,0:T(1,128)} %param.11) | copy-start | bytes 388
  116.6 13.9 %copy-start.46 = (s32[16,256]{1,0:T(8,128)S(1)}, s32[16,256]{1,0:T(8,128)}, u32[]{:S(2)}) copy-start(s32[16,256]{1,0:T(8,128)} %copy-done.45) | copy-start | bytes 49156
  116.6 20.2 %copy-start.40 = (s32[16,256]{1,0:T(8,128)S(1)}, s32[16,256]{1,0:T(8,128)}, u32[]{:S(2)}) copy-start(s32[16,256]{1,0:T(8,128)} %copy-done.38) | copy-start | bytes 49156
  117.3 15.3 %collective-permute-start.11 = (f32[3,16,16,3]{3,2,1,0:T(8,128)S(1)}, f32[3,16,16,3]{3,2,1,0:T(8,128)S(1)}, u32[]{:S(2)}, u32[]{:S(2)}) collective-permute-start(f32[3,16,16,3]{3,2,1,0:T(8,128)S(1)} %get-tuple-element.625), channel_id=1, source_target_pairs={{1,0},{2,1},{3,2},{4,3},{5,4},{6,5},{7,6},{9,8},{10,9},{11,10},{12... | collective-permute-start | bytes 27656 | tf_op jit(solution)/shard_map/ppermute | solution.py:48
  119.5 19.4 %collective-permute-start.10 = (f32[3,16,3,256]{3,2,1,0:T(4,128)S(1)}, f32[3,16,3,256]{3,2,1,0:T(4,128)S(1)}, u32[]{:S(2)}, u32[]{:S(2)}) collective-permute-start(f32[3,16,3,256]{3,2,1,0:T(4,128)S(1)} %get-tuple-element.627), channel_id=1, source_target_pairs={{8,0},{16,8},{24,16},{9,1},{17,9},{25,17},{10,2},{18,10},{26,18},{... | collective-permute-start | bytes 442376 | tf_op jit(solution)/shard_map/ppermute | solution.py:48
  120.8 18.1 %collective-permute-start.7 = (f32[3,16,3,256]{3,2,1,0:T(4,128)S(1)}, f32[3,16,3,256]{3,2,1,0:T(4,128)S(1)}, u32[]{:S(2)}, u32[]{:S(2)}) collective-permute-start(f32[3,16,3,256]{3,2,1,0:T(4,128)S(1)} %get-tuple-element.626), channel_id=1, source_target_pairs={{0,8},{8,16},{16,24},{1,9},{9,17},{17,25},{2,10},{10,18},{18,26},{... | collective-permute-start | bytes 442376 | tf_op jit(solution)/shard_map/ppermute | solution.py:47
  124.8 14.1 %collective-permute-start.6 = (f32[3,16,16,3]{3,2,1,0:T(8,128)S(1)}, f32[3,16,16,3]{3,2,1,0:T(8,128)S(1)}, u32[]{:S(2)}, u32[]{:S(2)}) collective-permute-start(f32[3,16,16,3]{3,2,1,0:T(8,128)S(1)} %get-tuple-element.624), channel_id=1, source_target_pairs={{0,1},{1,2},{2,3},{3,4},{4,5},{5,6},{6,7},{8,9},{9,10},{10,11},{11... | collective-permute-start | bytes 27656 | tf_op jit(solution)/shard_map/ppermute | solution.py:47
  128.7 10.3 %collective-permute-start.9 = (f32[3,3,16,256]{3,2,1,0:T(8,128)S(1)}, f32[3,3,16,256]{3,2,1,0:T(8,128)S(1)}, u32[]{:S(2)}, u32[]{:S(2)}) collective-permute-start(f32[3,3,16,256]{3,2,1,0:T(8,128)S(1)} %get-tuple-element.623), channel_id=1, source_target_pairs={{32,0},{64,32},{96,64},{33,1},{65,33},{97,65},{34,2},{66,34},{98,6... | collective-permute-start | bytes 442376 | tf_op jit(solution)/shard_map/ppermute | solution.py:48
  132.6 7.0 %collective-permute-start.8 = (f32[3,3,16,256]{3,2,1,0:T(8,128)S(1)}, f32[3,3,16,256]{3,2,1,0:T(8,128)S(1)}, u32[]{:S(2)}, u32[]{:S(2)}) collective-permute-start(f32[3,3,16,256]{3,2,1,0:T(8,128)S(1)} %get-tuple-element.622), channel_id=1, source_target_pairs={{0,32},{32,64},{64,96},{1,33},{33,65},{65,97},{2,34},{34,66},{66,9... | collective-permute-start | bytes 442376 | tf_op jit(solution)/shard_map/ppermute | solution.py:47
  155.1 24.9 %copy-start.47 = (s32[16,256]{1,0:T(8,128)S(1)}, s32[16,256]{1,0:T(8,128)}, u32[]{:S(2)}) copy-start(s32[16,256]{1,0:T(8,128)} %copy-done.45) | copy-start | bytes 49156
  155.1 34.5 %copy-start.36 = (s32[16]{0:T(128)S(1)}, s32[16]{0:T(128)}, u32[]{:S(2)}) copy-start(s32[16]{0:T(128)} %copy-done.35) | copy-start | bytes 196
  157.6 42.6 %copy-start.41 = (s32[16,256]{1,0:T(8,128)S(1)}, s32[16,256]{1,0:T(8,128)}, u32[]{:S(2)}) copy-start(s32[16,256]{1,0:T(8,128)} %copy-done.38) | copy-start | bytes 49156
  157.6 44.3 %copy-start.59 = (s32[16]{0:T(128)S(1)}, s32[16]{0:T(128)}, u32[]{:S(2)}) copy-start(s32[16]{0:T(128)} %get-tuple-element.655) | copy-start | bytes 196
  202.7 14.1 %copy-start.48 = (s32[16,256]{1,0:T(8,128)S(1)}, s32[16,256]{1,0:T(8,128)}, u32[]{:S(2)}) copy-start(s32[16,256]{1,0:T(8,128)} %copy-done.45) | copy-start | bytes 49156
  203.4 16.2 %collective-permute-start.17 = (f32[3,16,16,3]{3,2,1,0:T(8,128)S(1)}, f32[3,16,16,3]{3,2,1,0:T(8,128)S(1)}, u32[]{:S(2)}, u32[]{:S(2)}) collective-permute-start(f32[3,16,16,3]{3,2,1,0:T(8,128)S(1)} %get-tuple-element.617), channel_id=1, source_target_pairs={{1,0},{2,1},{3,2},{4,3},{5,4},{6,5},{7,6},{9,8},{10,9},{11,10},{12... | collective-permute-start | bytes 27656 | tf_op jit(solution)/shard_map/ppermute | solution.py:48
  205.7 20.7 %collective-permute-start.16 = (f32[3,16,3,256]{3,2,1,0:T(4,128)S(1)}, f32[3,16,3,256]{3,2,1,0:T(4,128)S(1)}, u32[]{:S(2)}, u32[]{:S(2)}) collective-permute-start(f32[3,16,3,256]{3,2,1,0:T(4,128)S(1)} %get-tuple-element.619), channel_id=1, source_target_pairs={{8,0},{16,8},{24,16},{9,1},{17,9},{25,17},{10,2},{18,10},{26,18},{... | collective-permute-start | bytes 442376 | tf_op jit(solution)/shard_map/ppermute | solution.py:48
  207.0 19.4 %collective-permute-start.13 = (f32[3,16,3,256]{3,2,1,0:T(4,128)S(1)}, f32[3,16,3,256]{3,2,1,0:T(4,128)S(1)}, u32[]{:S(2)}, u32[]{:S(2)}) collective-permute-start(f32[3,16,3,256]{3,2,1,0:T(4,128)S(1)} %get-tuple-element.618), channel_id=1, source_target_pairs={{0,8},{8,16},{16,24},{1,9},{9,17},{17,25},{2,10},{10,18},{18,26},{... | collective-permute-start | bytes 442376 | tf_op jit(solution)/shard_map/ppermute | solution.py:47
  211.3 15.1 %collective-permute-start.12 = (f32[3,16,16,3]{3,2,1,0:T(8,128)S(1)}, f32[3,16,16,3]{3,2,1,0:T(8,128)S(1)}, u32[]{:S(2)}, u32[]{:S(2)}) collective-permute-start(f32[3,16,16,3]{3,2,1,0:T(8,128)S(1)} %get-tuple-element.616), channel_id=1, source_target_pairs={{0,1},{1,2},{2,3},{3,4},{4,5},{5,6},{6,7},{8,9},{9,10},{10,11},{11... | collective-permute-start | bytes 27656 | tf_op jit(solution)/shard_map/ppermute | solution.py:47
  214.9 11.5 %collective-permute-start.15 = (f32[3,3,16,256]{3,2,1,0:T(8,128)S(1)}, f32[3,3,16,256]{3,2,1,0:T(8,128)S(1)}, u32[]{:S(2)}, u32[]{:S(2)}) collective-permute-start(f32[3,3,16,256]{3,2,1,0:T(8,128)S(1)} %get-tuple-element.615), channel_id=1, source_target_pairs={{32,0},{64,32},{96,64},{33,1},{65,33},{97,65},{34,2},{66,34},{98,6... | collective-permute-start | bytes 442376 | tf_op jit(solution)/shard_map/ppermute | solution.py:48
  219.6 7.2 %collective-permute-start.14 = (f32[3,3,16,256]{3,2,1,0:T(8,128)S(1)}, f32[3,3,16,256]{3,2,1,0:T(8,128)S(1)}, u32[]{:S(2)}, u32[]{:S(2)}) collective-permute-start(f32[3,3,16,256]{3,2,1,0:T(8,128)S(1)} %get-tuple-element.614), channel_id=1, source_target_pairs={{0,32},{32,64},{64,96},{1,33},{33,65},{65,97},{2,34},{34,66},{66,9... | collective-permute-start | bytes 442376 | tf_op jit(solution)/shard_map/ppermute | solution.py:47
  241.9 17.5 %copy-start.4 = (f32[16,4,256]{2,0,1:T(8,128)S(1)}, f32[16,4,256]{2,0,1:T(8,128)}, u32[]{:S(2)}) copy-start(f32[16,4,256]{2,0,1:T(8,128)} %copy-done.1) | copy-start | bytes 196612
  241.9 26.9 %copy-start.49 = (s32[16,256]{1,0:T(8,128)S(1)}, s32[16,256]{1,0:T(8,128)}, u32[]{:S(2)}) copy-start(s32[16,256]{1,0:T(8,128)} %copy-done.45) | copy-start | bytes 49156
  241.9 38.4 %copy-start.37 = (s32[16]{0:T(128)S(1)}, s32[16]{0:T(128)}, u32[]{:S(2)}) copy-start(s32[16]{0:T(128)} %copy-done.35) | copy-start | bytes 196
  244.5 46.5 %copy-start.42 = (s32[16,256]{1,0:T(8,128)S(1)}, s32[16,256]{1,0:T(8,128)}, u32[]{:S(2)}) copy-start(s32[16,256]{1,0:T(8,128)} %copy-done.38) | copy-start | bytes 49156
  244.5 48.1 %copy-start.60 = (s32[16]{0:T(128)S(1)}, s32[16]{0:T(128)}, u32[]{:S(2)}) copy-start(s32[16]{0:T(128)} %get-tuple-element.655) | copy-start | bytes 196
  293.2 13.7 %copy-start.34 = (s32[1,1,1,32]{3,2,1,0:T(1,128)S(1)}, s32[1,1,1,32]{3,2,1,0:T(1,128)}, u32[]{:S(2)}) copy-start(s32[1,1,1,32]{3,2,1,0:T(1,128)} %param.11) | copy-start | bytes 388
  293.4 13.9 %copy-start.50 = (s32[16,256]{1,0:T(8,128)S(1)}, s32[16,256]{1,0:T(8,128)}, u32[]{:S(2)}) copy-start(s32[16,256]{1,0:T(8,128)} %copy-done.45) | copy-start | bytes 49156
  293.4 20.7 %copy-start.43 = (s32[16,256]{1,0:T(8,128)S(1)}, s32[16,256]{1,0:T(8,128)}, u32[]{:S(2)}) copy-start(s32[16,256]{1,0:T(8,128)} %copy-done.38) | copy-start | bytes 49156
  294.2 16.0 %collective-permute-start.23 = (f32[3,16,16,3]{3,2,1,0:T(8,128)S(1)}, f32[3,16,16,3]{3,2,1,0:T(8,128)S(1)}, u32[]{:S(2)}, u32[]{:S(2)}) collective-permute-start(f32[3,16,16,3]{3,2,1,0:T(8,128)S(1)} %get-tuple-element.609), channel_id=1, source_target_pairs={{1,0},{2,1},{3,2},{4,3},{5,4},{6,5},{7,6},{9,8},{10,9},{11,10},{12... | collective-permute-start | bytes 27656 | tf_op jit(solution)/shard_map/ppermute | solution.py:48
  296.5 19.9 %collective-permute-start.22 = (f32[3,16,3,256]{3,2,1,0:T(4,128)S(1)}, f32[3,16,3,256]{3,2,1,0:T(4,128)S(1)}, u32[]{:S(2)}, u32[]{:S(2)}) collective-permute-start(f32[3,16,3,256]{3,2,1,0:T(4,128)S(1)} %get-tuple-element.611), channel_id=1, source_target_pairs={{8,0},{16,8},{24,16},{9,1},{17,9},{25,17},{10,2},{18,10},{26,18},{... | collective-permute-start | bytes 442376 | tf_op jit(solution)/shard_map/ppermute | solution.py:48
  297.8 18.6 %collective-permute-start.19 = (f32[3,16,3,256]{3,2,1,0:T(4,128)S(1)}, f32[3,16,3,256]{3,2,1,0:T(4,128)S(1)}, u32[]{:S(2)}, u32[]{:S(2)}) collective-permute-start(f32[3,16,3,256]{3,2,1,0:T(4,128)S(1)} %get-tuple-element.610), channel_id=1, source_target_pairs={{0,8},{8,16},{16,24},{1,9},{9,17},{17,25},{2,10},{10,18},{18,26},{... | collective-permute-start | bytes 442376 | tf_op jit(solution)/shard_map/ppermute | solution.py:47
  301.8 14.5 %collective-permute-start.18 = (f32[3,16,16,3]{3,2,1,0:T(8,128)S(1)}, f32[3,16,16,3]{3,2,1,0:T(8,128)S(1)}, u32[]{:S(2)}, u32[]{:S(2)}) collective-permute-start(f32[3,16,16,3]{3,2,1,0:T(8,128)S(1)} %get-tuple-element.608), channel_id=1, source_target_pairs={{0,1},{1,2},{2,3},{3,4},{4,5},{5,6},{6,7},{8,9},{9,10},{10,11},{11... | collective-permute-start | bytes 27656 | tf_op jit(solution)/shard_map/ppermute | solution.py:47
  305.6 10.7 %collective-permute-start.21 = (f32[3,3,16,256]{3,2,1,0:T(8,128)S(1)}, f32[3,3,16,256]{3,2,1,0:T(8,128)S(1)}, u32[]{:S(2)}, u32[]{:S(2)}) collective-permute-start(f32[3,3,16,256]{3,2,1,0:T(8,128)S(1)} %get-tuple-element.607), channel_id=1, source_target_pairs={{32,0},{64,32},{96,64},{33,1},{65,33},{97,65},{34,2},{66,34},{98,6... | collective-permute-start | bytes 442376 | tf_op jit(solution)/shard_map/ppermute | solution.py:48
  310.2 6.9 %collective-permute-start.20 = (f32[3,3,16,256]{3,2,1,0:T(8,128)S(1)}, f32[3,3,16,256]{3,2,1,0:T(8,128)S(1)}, u32[]{:S(2)}, u32[]{:S(2)}) collective-permute-start(f32[3,3,16,256]{3,2,1,0:T(8,128)S(1)} %get-tuple-element.606), channel_id=1, source_target_pairs={{0,32},{32,64},{64,96},{1,33},{33,65},{65,97},{2,34},{34,66},{66,9... | collective-permute-start | bytes 442376 | tf_op jit(solution)/shard_map/ppermute | solution.py:47
  332.7 25.0 %copy-start.51 = (s32[16,256]{1,0:T(8,128)S(1)}, s32[16,256]{1,0:T(8,128)}, u32[]{:S(2)}) copy-start(s32[16,256]{1,0:T(8,128)} %copy-done.45) | copy-start | bytes 49156
  335.2 43.5 %copy-start.44 = (s32[16,256]{1,0:T(8,128)S(1)}, s32[16,256]{1,0:T(8,128)}, u32[]{:S(2)}) copy-start(s32[16,256]{1,0:T(8,128)} %copy-done.38) | copy-start | bytes 49156
  335.2 45.2 %copy-start.61 = (s32[16]{0:T(128)S(1)}, s32[16]{0:T(128)}, u32[]{:S(2)}) copy-start(s32[16]{0:T(128)} %get-tuple-element.655) | copy-start | bytes 196
  381.2 13.9 %copy-start.52 = (s32[16,256]{1,0:T(8,128)S(1)}, s32[16,256]{1,0:T(8,128)}, u32[]{:S(2)}) copy-start(s32[16,256]{1,0:T(8,128)} %copy-done.45) | copy-start | bytes 49156
  381.9 16.0 %collective-permute-start.29 = (f32[3,16,16,3]{3,2,1,0:T(8,128)S(1)}, f32[3,16,16,3]{3,2,1,0:T(8,128)S(1)}, u32[]{:S(2)}, u32[]{:S(2)}) collective-permute-start(f32[3,16,16,3]{3,2,1,0:T(8,128)S(1)} %get-tuple-element.601), channel_id=1, source_target_pairs={{1,0},{2,1},{3,2},{4,3},{5,4},{6,5},{7,6},{9,8},{10,9},{11,10},{12... | collective-permute-start | bytes 27656 | tf_op jit(solution)/shard_map/ppermute | solution.py:48
  384.2 20.5 %collective-permute-start.28 = (f32[3,16,3,256]{3,2,1,0:T(4,128)S(1)}, f32[3,16,3,256]{3,2,1,0:T(4,128)S(1)}, u32[]{:S(2)}, u32[]{:S(2)}) collective-permute-start(f32[3,16,3,256]{3,2,1,0:T(4,128)S(1)} %get-tuple-element.603), channel_id=1, source_target_pairs={{8,0},{16,8},{24,16},{9,1},{17,9},{25,17},{10,2},{18,10},{26,18},{... | collective-permute-start | bytes 442376 | tf_op jit(solution)/shard_map/ppermute | solution.py:48
  385.5 19.2 %collective-permute-start.25 = (f32[3,16,3,256]{3,2,1,0:T(4,128)S(1)}, f32[3,16,3,256]{3,2,1,0:T(4,128)S(1)}, u32[]{:S(2)}, u32[]{:S(2)}) collective-permute-start(f32[3,16,3,256]{3,2,1,0:T(4,128)S(1)} %get-tuple-element.602), channel_id=1, source_target_pairs={{0,8},{8,16},{16,24},{1,9},{9,17},{17,25},{2,10},{10,18},{18,26},{... | collective-permute-start | bytes 442376 | tf_op jit(solution)/shard_map/ppermute | solution.py:47
  389.5 15.2 %collective-permute-start.24 = (f32[3,16,16,3]{3,2,1,0:T(8,128)S(1)}, f32[3,16,16,3]{3,2,1,0:T(8,128)S(1)}, u32[]{:S(2)}, u32[]{:S(2)}) collective-permute-start(f32[3,16,16,3]{3,2,1,0:T(8,128)S(1)} %get-tuple-element.600), channel_id=1, source_target_pairs={{0,1},{1,2},{2,3},{3,4},{4,5},{5,6},{6,7},{8,9},{9,10},{10,11},{11... | collective-permute-start | bytes 27656 | tf_op jit(solution)/shard_map/ppermute | solution.py:47
  393.4 11.3 %collective-permute-start.27 = (f32[3,3,16,256]{3,2,1,0:T(8,128)S(1)}, f32[3,3,16,256]{3,2,1,0:T(8,128)S(1)}, u32[]{:S(2)}, u32[]{:S(2)}) collective-permute-start(f32[3,3,16,256]{3,2,1,0:T(8,128)S(1)} %get-tuple-element.599), channel_id=1, source_target_pairs={{32,0},{64,32},{96,64},{33,1},{65,33},{97,65},{34,2},{66,34},{98,6... | collective-permute-start | bytes 442376 | tf_op jit(solution)/shard_map/ppermute | solution.py:48
  397.9 6.9 %collective-permute-start.26 = (f32[3,3,16,256]{3,2,1,0:T(8,128)S(1)}, f32[3,3,16,256]{3,2,1,0:T(8,128)S(1)}, u32[]{:S(2)}, u32[]{:S(2)}) collective-permute-start(f32[3,3,16,256]{3,2,1,0:T(8,128)S(1)} %get-tuple-element.598), channel_id=1, source_target_pairs={{0,32},{32,64},{64,96},{1,33},{33,65},{65,97},{2,34},{34,66},{66,9... | collective-permute-start | bytes 442376 | tf_op jit(solution)/shard_map/ppermute | solution.py:47
  422.5 51.7 %copy-start.7 = (f32[3,256,256]{1,2,0:T(8,128)S(1)}, f32[3,256,256]{1,2,0:T(8,128)}, u32[]{:S(2)}) copy-start(f32[3,256,256]{1,2,0:T(8,128)} %copy-done.6) | copy-start | bytes 2359300
  422.5 51.7 %copy-start.9 = (f32[3,256,256]{1,2,0:T(8,128)S(1)}, f32[3,256,256]{1,2,0:T(8,128)}, u32[]{:S(2)}) copy-start(f32[3,256,256]{1,2,0:T(8,128)} %copy-done.8) | copy-start | bytes 2359300
  422.5 51.7 %copy-start.11 = (f32[3,256,256]{1,2,0:T(8,128)S(1)}, f32[3,256,256]{1,2,0:T(8,128)}, u32[]{:S(2)}) copy-start(f32[3,256,256]{1,2,0:T(8,128)} %copy-done.10) | copy-start | bytes 2359300
  424.9 49.2 %copy-start.62 = (s32[16]{0:T(128)S(1)}, s32[16]{0:T(128)}, u32[]{:S(2)}) copy-start(s32[16]{0:T(128)} %get-tuple-element.655) | copy-start | bytes 196
  (34 other events, 164.8 us)
